TPU v7x, 32 devices: a whole 2x2x4 slice. The times are simulated.
32 devices in a mesh: ctx: 8 (over z, core), head: 4 (over y, x).
Axes of the slice: x: 2, y: 2, z: 4, core: 2. Of those that a mesh axis runs over, the one named last changes fastest.
Arguments:
- queries: bfloat16 [2048, 8192], P(('ctx', 'head')), may hold values from -100 to 100
- keys: bfloat16 [2048, 1024], P(('ctx', 'head')), may hold values from -100 to 100
- values: bfloat16 [2048, 1024], P(('ctx', 'head')), may hold values from -6 to 6
- out_grad: bfloat16 [2048, 8192], P(('ctx', 'head')), may hold values from -6 to 6
- doc_ids: int32 [2048], replicated, may hold values from 0 to 3, never falling along the last dimension, each value on 1 to 1024 neighbouring positions
Outputs:
- query_grad: float32 [2048, 8192], P(('ctx', 'head'))
- key_grad: float32 [2048, 1024], P(('ctx', 'head'))
- value_grad: float32 [2048, 1024], P(('ctx', 'head'))
Inputs may be any that keep to these rules, and one draw needn't show every extreme that they name: `doc_ids`: never falling along the sequence; each document holds 1 to 1024 tokens, one exactly 1024.
All inputs are finite; a program needn't handle non-finite values.
Results may differ from a plain program's by a relative error of at most 0.004.
Values may be sent and summed in bfloat16 or wider, within the bound.
A program may use at most 64 MiB of HBM per device.

v0:
```python
import jax
import jax.numpy as jnp
from jax import lax
from jax.sharding import PartitionSpec as P

HD = 128


def passed_along(array, axis, by):
    size = lax.axis_size(axis)
    pairs = [(i, i + by) for i in range(size) if 0 <= i + by < size]
    return lax.ppermute(array, axis, pairs)


def body(queries, keys, values, out_grad, doc_ids):
    head_count = lax.axis_size("head")
    row_count = queries.shape[0] * head_count
    score_scale = 1.0 / HD**0.5
    query_loc, key_loc, value_loc, grad_loc = (
        lax.all_to_all(queries, "head", split_axis=1, concat_axis=0, tiled=True),
        lax.all_to_all(keys, "head", split_axis=1, concat_axis=0, tiled=True),
        lax.all_to_all(values, "head", split_axis=1, concat_axis=0, tiled=True),
        lax.all_to_all(out_grad, "head", split_axis=1, concat_axis=0, tiled=True),
    )
    kv_local = key_loc.shape[1] // HD
    group_size = query_loc.shape[1] // key_loc.shape[1]
    key_value = jnp.stack([key_loc, value_loc])
    received = [key_value]
    current = key_value
    for stride in range(1, 4):
        current = passed_along(current, "ctx", 1)
        received.append(current)
    window_kv = jnp.concatenate(received[::-1], axis=1)
    key_win = window_kv[0].reshape(4 * row_count, kv_local, HD)
    value_win = window_kv[1].reshape(4 * row_count, kv_local, HD)
    first_row = lax.axis_index("ctx") * row_count
    query_pos = first_row + jnp.arange(row_count, dtype=jnp.int32)
    key_pos = first_row - 3 * row_count + jnp.arange(4 * row_count, dtype=jnp.int32)
    query_doc = lax.dynamic_slice_in_dim(doc_ids, first_row, row_count, 0)
    key_doc = jnp.concatenate(
        [
            lax.dynamic_slice_in_dim(
                doc_ids, jnp.maximum(first_row - stride * row_count, 0), row_count, 0
            )
            for stride in (3, 2, 1, 0)
        ],
        0,
    )
    allowed = (key_pos[None, :] <= query_pos[:, None]) & (
        key_pos[None, :] > query_pos[:, None] - 3 * row_count
    )
    allowed = allowed & (key_pos[None, :] >= 0) & (query_doc[:, None] == key_doc[None, :])
    query_heads = query_loc.reshape(row_count, kv_local, group_size, HD)
    scores = (
        jnp.einsum("ikgd,jkd->kgij", query_heads, key_win, preferred_element_type=jnp.float32)
        * score_scale
    )
    scores = jnp.where(allowed[None, None], scores, -jnp.inf)
    row_max = jnp.max(scores, -1, keepdims=True)
    expo = jnp.exp(scores - row_max)
    weights = expo / jnp.sum(expo, -1, keepdims=True)
    weight_bf = weights.astype(jnp.bfloat16)
    attended = jnp.einsum(
        "kgij,jkd->ikgd", weight_bf, value_win, preferred_element_type=jnp.float32
    )
    grad_heads = grad_loc.reshape(row_count, kv_local, group_size, HD)
    delta_sum = jnp.transpose(jnp.sum(grad_heads.astype(jnp.float32) * attended, -1), (1, 2, 0))
    value_part = jnp.einsum(
        "kgij,ikgd->jkd", weight_bf, grad_heads, preferred_element_type=jnp.float32
    )
    prob_grad = jnp.einsum(
        "ikgd,jkd->kgij", grad_heads, value_win, preferred_element_type=jnp.float32
    )
    score_grad = (weights * (prob_grad - delta_sum[..., None])).astype(jnp.bfloat16)
    query_full = (
        jnp.einsum("kgij,jkd->ikgd", score_grad, key_win, preferred_element_type=jnp.float32)
        * score_scale
    )
    key_part = (
        jnp.einsum("kgij,ikgd->jkd", score_grad, query_heads, preferred_element_type=jnp.float32)
        * score_scale
    )
    partials = jnp.stack([key_part, value_part]).reshape(2, 4 * row_count, kv_local * HD)

    def piece(stride):
        return partials[:, (3 - stride) * row_count : (4 - stride) * row_count]

    total = piece(3)
    for stride in (2, 1, 0):
        total = passed_along(total, "ctx", -1) + piece(stride)
    query_rows = query_full.reshape(row_count, -1)
    query_back, key_back, value_back = (
        lax.all_to_all(query_rows, "head", split_axis=0, concat_axis=1, tiled=True),
        lax.all_to_all(total[0], "head", split_axis=0, concat_axis=1, tiled=True),
        lax.all_to_all(total[1], "head", split_axis=0, concat_axis=1, tiled=True),
    )
    return (query_back, key_back, value_back)


def solution(mesh):
    return jax.shard_map(
        body,
        mesh=mesh,
        in_specs=(
            P(("ctx", "head"), None),
            P(("ctx", "head"), None),
            P(("ctx", "head"), None),
            P(("ctx", "head"), None),
            P(),
        ),
        out_specs=(P(("ctx", "head"), None), P(("ctx", "head"), None), P(("ctx", "head"), None)),
        check_vma=False,
    )
```

profile of v0, /device:TPU:8, one launch (start us, length us, event | category | flops | bytes accessed | tf_op | source)
XLA Modules:
  0.0 173.3 jit_solution(2294293589609892568)
XLA Ops:
  2.2 3.7 %all-to-all-start = ((bf16[64,4,256]{2,0,1:T(8,128)(2,1)}), bf16[64,4,256]{2,0,1:T(8,128)(2,1)S(1)}, u32[]{:S(2)}, u32[]{:S(2)}) async-start(bf16[64,4,256]{2,0,1:T(8,128)(2,1)} %bitcast.112), calls=%async_computation | async-start | bytes 262144 | tf_op jit(solution)/shard_map/all_to_all | solution.py:21
  7.5 3.5 %all-to-all-done = bf16[64,4,256]{2,0,1:T(8,128)(2,1)S(1)} async-done(((bf16[64,4,256]{2,0,1:T(8,128)(2,1)}), bf16[64,4,256]{2,0,1:T(8,128)(2,1)S(1)}, u32[]{:S(2)}, u32[]{:S(2)}) %all-to-all-start) | async-done | bytes 131104 | tf_op jit(solution)/shard_map/all_to_all | solution.py:21
  11.0 3.3 %all-to-all-start.1 = ((bf16[64,4,256]{2,0,1:T(8,128)(2,1)}), bf16[64,4,256]{2,0,1:T(8,128)(2,1)S(1)}, u32[]{:S(2)}, u32[]{:S(2)}) async-start(bf16[64,4,256]{2,0,1:T(8,128)(2,1)} %bitcast.111), calls=%async_computation.1 | async-start | bytes 262144 | tf_op jit(solution)/shard_map/all_to_all | solution.py:22
  14.3 2.3 %copy.112 = bf16[8,4,8,2048]{3,2,0,1:T(8,128)(2,1)} copy(bf16[8,4,8,2048]{3,2,1,0:T(8,128)(2,1)} %bitcast.128) | data formatting | bytes 2097152 | tf_op jit(solution)/shard_map/all_to_all | solution.py:20
  16.6 2.7 %all-to-all-done.1 = bf16[64,4,256]{2,0,1:T(8,128)(2,1)S(1)} async-done(((bf16[64,4,256]{2,0,1:T(8,128)(2,1)}), bf16[64,4,256]{2,0,1:T(8,128)(2,1)S(1)}, u32[]{:S(2)}, u32[]{:S(2)}) %all-to-all-start.1) | async-done | bytes 131104 | tf_op jit(solution)/shard_map/all_to_all | solution.py:22
  19.3 3.5 %all-to-all-start.2 = ((bf16[64,4,2048]{2,0,1:T(8,128)(2,1)}), bf16[64,4,2048]{2,0,1:T(8,128)(2,1)S(1)}, u32[]{:S(2)}, u32[]{:S(2)}) async-start(bf16[64,4,2048]{2,0,1:T(8,128)(2,1)} %bitcast.110), calls=%async_computation.2 | async-start | bytes 2097152 | tf_op jit(solution)/shard_map/all_to_all | solution.py:20
  22.8 1.9 %collective-permute-start = (bf16[2,256,256]{2,1,0:T(8,128)(2,1)S(1)}, bf16[2,256,256]{2,1,0:T(8,128)(2,1)S(1)}, u32[]{:S(2)}, u32[]{:S(2)}) collective-permute-start(bf16[2,256,256]{2,1,0:T(8,128)(2,1)S(1)} %pad_maximum_fusion.1), channel_id=1, source_target_pairs={{0,4},{4,8},{8,12},{12,16},{16,20},{20,24},{24,28},{1,5},{5,9},{9,... | collective-permute-start | bytes 786440 | tf_op jit(solution)/shard_map/ppermute | solution.py:12
  24.8 2.3 %copy.111 = bf16[8,4,8,2048]{3,2,0,1:T(8,128)(2,1)} copy(bf16[8,4,8,2048]{3,2,1,0:T(8,128)(2,1)} %bitcast.129) | data formatting | bytes 2097152 | tf_op jit(solution)/shard_map/all_to_all | solution.py:23
  27.1 7.0 %all-to-all-done.2 = bf16[64,4,2048]{2,0,1:T(8,128)(2,1)S(1)} async-done(((bf16[64,4,2048]{2,0,1:T(8,128)(2,1)}), bf16[64,4,2048]{2,0,1:T(8,128)(2,1)S(1)}, u32[]{:S(2)}, u32[]{:S(2)}) %all-to-all-start.2) | async-done | bytes 1048608 | tf_op jit(solution)/shard_map/all_to_all | solution.py:20
  34.1 3.5 %all-to-all-start.3 = ((bf16[64,4,2048]{2,0,1:T(8,128)(2,1)}), bf16[64,4,2048]{2,0,1:T(8,128)(2,1)S(1)}, u32[]{:S(2)}, u32[]{:S(2)}) async-start(bf16[64,4,2048]{2,0,1:T(8,128)(2,1)} %bitcast.109), calls=%async_computation.3 | async-start | bytes 2097152 | tf_op jit(solution)/shard_map/all_to_all | solution.py:23
  37.7 1.9 %collective-permute-start.1 = (bf16[2,256,256]{2,1,0:T(8,128)(2,1)S(1)}, bf16[2,256,256]{2,1,0:T(8,128)(2,1)}, u32[]{:S(2)}, u32[]{:S(2)}) collective-permute-start(bf16[2,256,256]{2,1,0:T(8,128)(2,1)S(1)} %collective-permute-done), channel_id=1, source_target_pairs={{0,4},{4,8},{8,12},{12,16},{16,20},{20,24},{24,28},{1,5},{5,9},{9,... | collective-permute-start | bytes 786440 | tf_op jit(solution)/shard_map/ppermute | solution.py:12
  39.7 5.7 %collective-permute-done.1 = bf16[2,256,256]{2,1,0:T(8,128)(2,1)} collective-permute-done((bf16[2,256,256]{2,1,0:T(8,128)(2,1)S(1)}, bf16[2,256,256]{2,1,0:T(8,128)(2,1)}, u32[]{:S(2)}, u32[]{:S(2)}) %collective-permute-start.1) | collective-permute-done | bytes 262176 | tf_op jit(solution)/shard_map/ppermute | solution.py:12
  57.1 2.1 %copy.63 = bf16[1,1024,256]{1,2,0:T(8,128)(2,1)} copy(bf16[1,1024,256]{2,1,0:T(8,128)(2,1)} %get-tuple-element.4) | data formatting | bytes 1048576 | tf_op jit(solution)/shard_map/slice | solution.py:34
  59.2 9.6 %fusion.23 = (f32[2,8,256]{2,1,0:T(8,128)S(1)}, f32[2,8,256,1024]{2,3,1,0:T(8,128)}) fusion(pred[256,1024]{0,1:T(8,128)(4,1)S(1)} %copy-done.3, bf16[1024,2,128,1]{0,2,3,1:T(8,128)(2,1)} %bitcast.122, bf16[256,2,8,128]{0,3,2,1:T(8,128)(2,1)S(1)} %copy.77), kind=kOutput, calls=%fused_computation.48 | convolution fusion | flops 1090520064 | bytes 18628608 | tf_op jit(solution)/shard_map/sub | solution.py:60
  68.8 6.6 %fusion.7 = bf16[2,8,256,1024]{2,3,1,0:T(8,128)(2,1)S(1)} fusion(f32[2,8,256,1024]{2,3,1,0:T(8,128)} %get-tuple-element.13, f32[2,8,256]{2,1,0:T(8,128)S(1)} %get-tuple-element.12), kind=kLoop, calls=%fused_computation.11 | loop fusion | flops 8388608 | bytes 25182208 | tf_op jit(solution)/shard_map/convert_element_type | solution.py:62
  75.4 3.8 %fusion.24 = f32[2,1024,128,1]{1,2,3,0:T(8,128)} fusion(bf16[2,8,256,1024]{2,3,1,0:T(8,128)(2,1)S(1)} %fusion.7, bf16[256,2,8,128]{0,3,2,1:T(8,128)(2,1)S(1)} %copy.71), kind=kOutput, calls=%fused_computation.49 | convolution fusion | flops 1073741824 | bytes 10485760 | tf_op jit(solution)/shard_map/kgij,ikgd->jkd/dot_general | solution.py:68
  82.1 7.1 %fusion.2 = bf16[2,8,256,1024]{2,3,1,0:T(8,128)(2,1)S(1)} fusion(f32[2,8,256]{2,1,0:T(8,128)S(1)} %bitcast.137, f32[2,8,256,1024]{2,3,1,0:T(8,128)} %get-tuple-element.13, f32[2,8,256]{2,1,0:T(8,128)S(1)} %get-tuple-element.12, bf16[1024,2,128,1]{0,2,3,1:T(8,128)(2,1)S(1)} %bitcast.120, bf16[256,2,8,128]{0,3,2,1:T(8,128)(2,1)S(1)} %copy.71), kind=kOutput, calls=%fused_computation.3 | convolution fusion | flops 1090519040 | bytes 26771456 | tf_op jit(solution)/shard_map/ikgd,jkd->kgij/dot_general | solution.py:71
  89.2 3.2 %copy-done = bf16[2,8,256,1024]{2,3,1,0:T(8,128)(2,1)} copy-done((bf16[2,8,256,1024]{2,3,1,0:T(8,128)(2,1)}, bf16[2,8,256,1024]{2,3,1,0:T(8,128)(2,1)S(1)}, u32[]{:S(2)}) %copy-start) | copy-done | bytes 8388632
  92.5 5.1 %fusion.11 = f32[2,1024,128]{1,2,0:T(8,128)} fusion(bf16[2,8,256,1024]{2,3,1,0:T(8,128)(2,1)S(1)} %fusion.2, bf16[256,2,8,128]{0,3,2,1:T(8,128)(2,1)} %copy-done.1), kind=kOutput, calls=%fused_computation.23 | convolution fusion | flops 1074003968 | bytes 10485760 | tf_op jit(solution)/shard_map/kgij,ikgd->jkd/dot_general | solution.py:80
  99.2 3.0 %collective-permute-start.3 = (f32[2,256,256]{2,1,0:T(8,128)S(1)}, f32[2,256,256]{2,1,0:T(8,128)S(1)}, u32[]{:S(2)}, u32[]{:S(2)}) collective-permute-start(f32[2,256,256]{2,1,0:T(8,128)S(1)} %fusion.14), channel_id=1, source_target_pairs={{4,0},{8,4},{12,8},{16,12},{20,16},{24,20},{28,24},{5,1},{9,5},{13... | collective-permute-start | bytes 1572872 | tf_op jit(solution)/shard_map/ppermute | solution.py:12
  102.1 6.7 %collective-permute-done.3 = f32[2,256,256]{2,1,0:T(8,128)S(1)} collective-permute-done((f32[2,256,256]{2,1,0:T(8,128)S(1)}, f32[2,256,256]{2,1,0:T(8,128)S(1)}, u32[]{:S(2)}, u32[]{:S(2)}) %collective-permute-start.3) | collective-permute-done | bytes 524320 | tf_op jit(solution)/shard_map/ppermute | solution.py:12
  109.8 4.0 %collective-permute-start.4 = (f32[2,256,256]{2,1,0:T(8,128)}, f32[2,256,256]{2,1,0:T(8,128)}, u32[]{:S(2)}, u32[]{:S(2)}) collective-permute-start(f32[2,256,256]{2,1,0:T(8,128)} %fusion.16), channel_id=1, source_target_pairs={{4,0},{8,4},{12,8},{16,12},{20,16},{24,20},{28,24},{5,1},{9,5},{13... | collective-permute-start | bytes 1572872 | tf_op jit(solution)/shard_map/ppermute | solution.py:12
  113.8 6.0 %multiply_bitcast_fusion = f32[256,2,8,128]{0,3,2,1:T(8,128)} fusion(bf16[1024,2,128,1]{0,2,3,1:T(8,128)(2,1)S(1)} %bitcast.123, bf16[2,8,256,1024]{2,3,1,0:T(8,128)(2,1)} %copy-done), kind=kOutput, calls=%fused_computation.20 | convolution fusion | flops 1074266112 | bytes 11010048 | tf_op jit(solution)/shard_map/kgij,jkd->ikgd/dot_general | solution.py:76
  119.8 3.0 %copy.74 = f32[256,2,8,128]{3,2,1,0:T(8,128)} copy(f32[256,2,8,128]{0,3,2,1:T(8,128)} %multiply_bitcast_fusion) | data formatting | bytes 4194304 | tf_op jit(solution)/shard_map/mul | solution.py:76
  122.8 2.7 %all_to_all.102 = f32[4,64,2048]{2,1,0:T(8,128)} reshape(f32[256,2,8,128]{3,2,1,0:T(8,128)} %copy.74) | data formatting | bytes 4194304 | tf_op jit(solution)/shard_map/all_to_all | solution.py:93
  125.5 4.5 %all-to-all-start.4 = ((f32[4,64,2048]{2,1,0:T(8,128)}), f32[4,64,2048]{2,1,0:T(8,128)}, u32[]{:S(2)}, u32[]{:S(2)}) async-start(f32[4,64,2048]{2,1,0:T(8,128)} %all_to_all.102), calls=%async_computation.4 | async-start | bytes 4194304 | tf_op jit(solution)/shard_map/all_to_all | solution.py:93
  131.1 1.9 %collective-permute-start.5 = (f32[2,256,256]{2,1,0:T(8,128)S(1)}, f32[2,256,256]{2,1,0:T(8,128)S(1)}, u32[]{:S(2)}, u32[]{:S(2)}) collective-permute-start(f32[2,256,256]{2,1,0:T(8,128)S(1)} %fusion.13), channel_id=1, source_target_pairs={{4,0},{8,4},{12,8},{16,12},{20,16},{24,20},{28,24},{5,1},{9,5},{13... | collective-permute-start | bytes 1572872 | tf_op jit(solution)/shard_map/ppermute | solution.py:12
  133.0 6.7 %collective-permute-done.5 = f32[2,256,256]{2,1,0:T(8,128)S(1)} collective-permute-done((f32[2,256,256]{2,1,0:T(8,128)S(1)}, f32[2,256,256]{2,1,0:T(8,128)S(1)}, u32[]{:S(2)}, u32[]{:S(2)}) %collective-permute-start.5) | collective-permute-done | bytes 524320 | tf_op jit(solution)/shard_map/ppermute | solution.py:12
  140.5 15.0 %all-to-all-done.4 = f32[4,64,2048]{2,1,0:T(8,128)} async-done(((f32[4,64,2048]{2,1,0:T(8,128)}), f32[4,64,2048]{2,1,0:T(8,128)}, u32[]{:S(2)}, u32[]{:S(2)}) %all-to-all-start.4) | async-done | bytes 2097184 | tf_op jit(solution)/shard_map/all_to_all | solution.py:93
  155.5 8.3 %all_to_all.121 = f32[4,64,256]{2,1,0:T(8,128)S(1)} all-to-all(f32[4,64,256]{2,1,0:T(8,128)S(1)} %bitcast.132), channel_id=1, replica_groups=mesh['ctx'=8,'head'=4] {'head'}, dimensions={0} | all-to-all | bytes 524288 | tf_op jit(solution)/shard_map/all_to_all | solution.py:94
  163.8 3.4 %all-to-all-start.6 = ((f32[4,64,256]{2,1,0:T(8,128)}), f32[4,64,256]{2,1,0:T(8,128)S(1)}, u32[]{:S(2)}, u32[]{:S(2)}) async-start(f32[4,64,256]{2,1,0:T(8,128)} %bitcast.30), calls=%async_computation.6 | async-start | bytes 524288 | tf_op jit(solution)/shard_map/all_to_all | solution.py:95
  167.2 3.1 %copy.102 = f32[4,8,8,2048]{3,2,0,1:T(8,128)} copy(f32[4,8,8,2048]{3,2,1,0:T(8,128)} %bitcast.53) | data formatting | bytes 4194304 | tf_op jit(solution)/shard_map/all_to_all | solution.py:93
  (42 shorter events, 25.2 us)
Async XLA Ops:
  0.6 39.0 %copy-start.5 = (s32[2048]{0:T(1024)S(1)}, s32[2048]{0:T(1024)}, u32[]{:S(2)}) copy-start(s32[2048]{0:T(1024)} %param.9) | copy-start | bytes 24580
  2.2 8.7 %all-to-all-start = ((bf16[64,4,256]{2,0,1:T(8,128)(2,1)}), bf16[64,4,256]{2,0,1:T(8,128)(2,1)S(1)}, u32[]{:S(2)}, u32[]{:S(2)}) async-start(bf16[64,4,256]{2,0,1:T(8,128)(2,1)} %bitcast.112), calls=%async_computation | async-start | bytes 262144 | tf_op jit(solution)/shard_map/all_to_all | solution.py:21
  11.0 8.3 %all-to-all-start.1 = ((bf16[64,4,256]{2,0,1:T(8,128)(2,1)}), bf16[64,4,256]{2,0,1:T(8,128)(2,1)S(1)}, u32[]{:S(2)}, u32[]{:S(2)}) async-start(bf16[64,4,256]{2,0,1:T(8,128)(2,1)} %bitcast.111), calls=%async_computation.1 | async-start | bytes 262144 | tf_op jit(solution)/shard_map/all_to_all | solution.py:22
  19.3 14.8 %all-to-all-start.2 = ((bf16[64,4,2048]{2,0,1:T(8,128)(2,1)}), bf16[64,4,2048]{2,0,1:T(8,128)(2,1)S(1)}, u32[]{:S(2)}, u32[]{:S(2)}) async-start(bf16[64,4,2048]{2,0,1:T(8,128)(2,1)} %bitcast.110), calls=%async_computation.2 | async-start | bytes 2097152 | tf_op jit(solution)/shard_map/all_to_all | solution.py:20
  22.8 14.8 %collective-permute-start = (bf16[2,256,256]{2,1,0:T(8,128)(2,1)S(1)}, bf16[2,256,256]{2,1,0:T(8,128)(2,1)S(1)}, u32[]{:S(2)}, u32[]{:S(2)}) collective-permute-start(bf16[2,256,256]{2,1,0:T(8,128)(2,1)S(1)} %pad_maximum_fusion.1), channel_id=1, source_target_pairs={{0,4},{4,8},{8,12},{12,16},{16,20},{20,24},{24,28},{1,5},{5,9},{9,... | collective-permute-start | bytes 786440 | tf_op jit(solution)/shard_map/ppermute | solution.py:12
  34.1 16.6 %all-to-all-start.3 = ((bf16[64,4,2048]{2,0,1:T(8,128)(2,1)}), bf16[64,4,2048]{2,0,1:T(8,128)(2,1)S(1)}, u32[]{:S(2)}, u32[]{:S(2)}) async-start(bf16[64,4,2048]{2,0,1:T(8,128)(2,1)} %bitcast.109), calls=%async_computation.3 | async-start | bytes 2097152 | tf_op jit(solution)/shard_map/all_to_all | solution.py:23
  37.6 11.3 %copy-start.4 = (bf16[2,256,256]{2,1,0:T(8,128)(2,1)}, bf16[2,256,256]{2,1,0:T(8,128)(2,1)S(1)}, u32[]{:S(2)}) copy-start(bf16[2,256,256]{2,1,0:T(8,128)(2,1)S(1)} %collective-permute-done) | copy-start | bytes 786436
  37.7 7.8 %collective-permute-start.1 = (bf16[2,256,256]{2,1,0:T(8,128)(2,1)S(1)}, bf16[2,256,256]{2,1,0:T(8,128)(2,1)}, u32[]{:S(2)}, u32[]{:S(2)}) collective-permute-start(bf16[2,256,256]{2,1,0:T(8,128)(2,1)S(1)} %collective-permute-done), channel_id=1, source_target_pairs={{0,4},{4,8},{8,12},{12,16},{16,20},{20,24},{24,28},{1,5},{5,9},{9,... | collective-permute-start | bytes 786440 | tf_op jit(solution)/shard_map/ppermute | solution.py:12
  45.4 8.2 %collective-permute-start.2 = (bf16[2,256,256]{2,1,0:T(8,128)(2,1)}, bf16[2,256,256]{2,1,0:T(8,128)(2,1)}, u32[]{:S(2)}, u32[]{:S(2)}) collective-permute-start(bf16[2,256,256]{2,1,0:T(8,128)(2,1)} %collective-permute-done.1), channel_id=1, source_target_pairs={{0,4},{4,8},{8,12},{12,16},{16,20},{20,24},{24,28},{1,5},{5,9},{9,... | collective-permute-start | bytes 786440 | tf_op jit(solution)/shard_map/ppermute | solution.py:12
  50.0 18.8 %copy-start.1 = (bf16[256,2,8,128]{0,3,2,1:T(8,128)(2,1)}, bf16[256,2,8,128]{0,3,2,1:T(8,128)(2,1)S(1)}, u32[]{:S(2)}) copy-start(bf16[256,2,8,128]{0,3,2,1:T(8,128)(2,1)S(1)} %copy.77) | copy-start | bytes 3145732
  51.9 7.2 %copy-start.3 = (pred[256,1024]{0,1:T(8,128)(4,1)S(1)}, pred[256,1024]{0,1:T(8,128)(4,1)}, u32[]{:S(2)}) copy-start(pred[256,1024]{0,1:T(8,128)(4,1)} %compare_and_fusion) | copy-start | bytes 786436
  89.2 3.2 %copy-start = (bf16[2,8,256,1024]{2,3,1,0:T(8,128)(2,1)}, bf16[2,8,256,1024]{2,3,1,0:T(8,128)(2,1)S(1)}, u32[]{:S(2)}) copy-start(bf16[2,8,256,1024]{2,3,1,0:T(8,128)(2,1)S(1)} %fusion.2) | copy-start | bytes 25165828
  92.5 21.3 %copy-start.2 = (bf16[1,1024,256]{1,2,0:T(8,128)(2,1)S(1)}, bf16[1,1024,256]{1,2,0:T(8,128)(2,1)}, u32[]{:S(2)}) copy-start(bf16[1,1024,256]{1,2,0:T(8,128)(2,1)} %copy.63) | copy-start | bytes 1572868
  99.2 9.7 %collective-permute-start.3 = (f32[2,256,256]{2,1,0:T(8,128)S(1)}, f32[2,256,256]{2,1,0:T(8,128)S(1)}, u32[]{:S(2)}, u32[]{:S(2)}) collective-permute-start(f32[2,256,256]{2,1,0:T(8,128)S(1)} %fusion.14), channel_id=1, source_target_pairs={{4,0},{8,4},{12,8},{16,12},{20,16},{24,20},{28,24},{5,1},{9,5},{13... | collective-permute-start | bytes 1572872 | tf_op jit(solution)/shard_map/ppermute | solution.py:12
  109.8 20.2 %collective-permute-start.4 = (f32[2,256,256]{2,1,0:T(8,128)}, f32[2,256,256]{2,1,0:T(8,128)}, u32[]{:S(2)}, u32[]{:S(2)}) collective-permute-start(f32[2,256,256]{2,1,0:T(8,128)} %fusion.16), channel_id=1, source_target_pairs={{4,0},{8,4},{12,8},{16,12},{20,16},{24,20},{28,24},{5,1},{9,5},{13... | collective-permute-start | bytes 1572872 | tf_op jit(solution)/shard_map/ppermute | solution.py:12
  125.5 30.0 %all-to-all-start.4 = ((f32[4,64,2048]{2,1,0:T(8,128)}), f32[4,64,2048]{2,1,0:T(8,128)}, u32[]{:S(2)}, u32[]{:S(2)}) async-start(f32[4,64,2048]{2,1,0:T(8,128)} %all_to_all.102), calls=%async_computation.4 | async-start | bytes 4194304 | tf_op jit(solution)/shard_map/all_to_all | solution.py:93
  131.1 8.6 %collective-permute-start.5 = (f32[2,256,256]{2,1,0:T(8,128)S(1)}, f32[2,256,256]{2,1,0:T(8,128)S(1)}, u32[]{:S(2)}, u32[]{:S(2)}) collective-permute-start(f32[2,256,256]{2,1,0:T(8,128)S(1)} %fusion.13), channel_id=1, source_target_pairs={{4,0},{8,4},{12,8},{16,12},{20,16},{24,20},{28,24},{5,1},{9,5},{13... | collective-permute-start | bytes 1572872 | tf_op jit(solution)/shard_map/ppermute | solution.py:12
  163.8 8.8 %all-to-all-start.6 = ((f32[4,64,256]{2,1,0:T(8,128)}), f32[4,64,256]{2,1,0:T(8,128)S(1)}, u32[]{:S(2)}, u32[]{:S(2)}) async-start(f32[4,64,256]{2,1,0:T(8,128)} %bitcast.30), calls=%async_computation.6 | async-start | bytes 524288 | tf_op jit(solution)/shard_map/all_to_all | solution.py:95
where the time goes:
time: 175 us; the launch traced here: 173 us
  waiting for transfers between devices  49.4 us (28%)
  starting transfers between devices  36.6 us (21%)
  local copies, waits for them, and re-layouts  33.5 us (19%)
  matrix products  32.9 us (19%)
  other arithmetic  11.6 us (7%)
  blocking collectives  8.28 us (5%)
    ppermute x6, waiting for transfers between devices, passed_along(): return lax.ppermute(array, axis, pairs)  19.1 us
    all_to_all x1, waiting for transfers between devices, body(): lax.all_to_all(query_rows, 'head', split_axis=0, concat_axis=1, tiled=True)  15 us
    ppermute x6, starting transfers between devices, passed_along(): return lax.ppermute(array, axis, pairs)  14.6 us
    sub x1, matrix products, body(): expo = jnp.exp(scores - row_max)  9.64 us
    all_to_all x1, blocking collectives, body(): lax.all_to_all(total[0], 'head', split_axis=0, concat_axis=1, tiled=True)  8.28 us
    dot_general x1, matrix products, body(): jnp.einsum('ikgd,jkd->kgij', grad_heads, value_win, preferred_element_typ...  7.12 us
    all_to_all x1, waiting for transfers between devices, body(): lax.all_to_all(queries, 'head', split_axis=1, concat_axis=0, tiled=True)  7.03 us
    convert_element_type x1, other arithmetic, body(): weight_bf = weights.astype(jnp.bfloat16)  6.62 us
  transfers between devices with their start and end apart: 12, of which 9 were waited for; matrix products, arithmetic and copies ran while one was open for 15% of the time, Pallas kernels for 0%

commit v1 on v0

--- a/solution.py
+++ b/solution.py
@@ -91,7 +91,12 @@
     query_rows = query_full.reshape(row_count, -1)
     query_back, key_back, value_back = (
         lax.all_to_all(query_rows, "head", split_axis=0, concat_axis=1, tiled=True),
-        lax.all_to_all(total[0], "head", split_axis=0, concat_axis=1, tiled=True),
+        jnp.concatenate(
+            lax.all_to_all(
+                jnp.stack(jnp.split(total[0], lax.axis_size("head"), axis=0)), "head", 0, 0
+            ),
+            axis=1,
+        ),
         lax.all_to_all(total[1], "head", split_axis=0, concat_axis=1, tiled=True),
     )
     return (query_back, key_back, value_back)

time: 175 us -> 165 us (0.943)
  blocking collectives: 8.28 us -> 0 us
  waiting for transfers between devices: 49.4 us -> 43.1 us
  starting transfers between devices: 36.6 us -> 40.4 us
    all_to_all x1, waiting for transfers between devices: 15 us -> 4.02 us  [body(): lax.all_to_all(query_rows, 'head', split_axis=0, concat_axis=1, tiled=True)]
    all_to_all x1 -> x0, blocking collectives: 8.28 us -> none  [body(): lax.all_to_all(total[0], 'head', split_axis=0, concat_axis=1, tiled=True)]
    all_to_all x0 -> x1, starting transfers between devices: none -> 3.41 us  [body(): lax.all_to_all(jnp.stack(jnp.split(total[0], lax.axis_size('head'), axis=...]
    all_to_all x1, waiting for transfers between devices: 1.48 us -> 4.59 us  [body(): lax.all_to_all(total[1], 'head', split_axis=0, concat_axis=1, tiled=True)]
  transfers between devices with their start and end apart: 12 -> 13, of which waited for: 9 -> 10; matrix products, arithmetic and copies ran while one was open for 15% -> 17% of each run, Pallas kernels for 0% -> 0%
where the time goes in v1:
time: 165 us; the launch traced here: 163 us
  waiting for transfers between devices  43.1 us (26%)
  starting transfers between devices  40.4 us (24%)
  local copies, waits for them, and re-layouts  33.5 us (20%)
  matrix products  32.9 us (20%)
  other arithmetic  12.3 us (7%)
    ppermute x6, waiting for transfers between devices, passed_along(): return lax.ppermute(array, axis, pairs)  19.1 us
    ppermute x6, starting transfers between devices, passed_along(): return lax.ppermute(array, axis, pairs)  15 us
    sub x1, matrix products, body(): expo = jnp.exp(scores - row_max)  9.62 us
    dot_general x1, matrix products, body(): jnp.einsum('ikgd,jkd->kgij', grad_heads, value_win, preferred_element_typ...  7.11 us
    all_to_all x1, waiting for transfers between devices, body(): lax.all_to_all(queries, 'head', split_axis=1, concat_axis=0, tiled=True)  7.03 us
    convert_element_type x1, other arithmetic, body(): weight_bf = weights.astype(jnp.bfloat16)  6.62 us
    dot_general x1, matrix products, body(): jnp.einsum('kgij,jkd->ikgd', score_grad, key_win, preferred_element_type=...  6 us
    all_to_all x2, local copies, waits for them, and re-layouts, body(): lax.all_to_all(query_rows, 'head', split_axis=0, concat_axis=1, tiled=True)  5.84 us
  transfers between devices with their start and end apart: 13, of which 10 were waited for; matrix products, arithmetic and copies ran while one was open for 17% of the time, Pallas kernels for 0%

profile of v1, /device:TPU:8, one launch (start us, length us, event | category | flops | bytes accessed | tf_op | source)
XLA Modules:
  0.0 163.1 jit_solution(17773292918229964597)
XLA Ops:
  2.2 3.7 %all-to-all-start = ((bf16[64,4,256]{2,0,1:T(8,128)(2,1)}), bf16[64,4,256]{2,0,1:T(8,128)(2,1)S(1)}, u32[]{:S(2)}, u32[]{:S(2)}) async-start(bf16[64,4,256]{2,0,1:T(8,128)(2,1)} %bitcast.111), calls=%async_computation | async-start | bytes 262144 | tf_op jit(solution)/shard_map/all_to_all | solution.py:21
  7.5 3.5 %all-to-all-done = bf16[64,4,256]{2,0,1:T(8,128)(2,1)S(1)} async-done(((bf16[64,4,256]{2,0,1:T(8,128)(2,1)}), bf16[64,4,256]{2,0,1:T(8,128)(2,1)S(1)}, u32[]{:S(2)}, u32[]{:S(2)}) %all-to-all-start) | async-done | bytes 131104 | tf_op jit(solution)/shard_map/all_to_all | solution.py:21
  11.0 3.3 %all-to-all-start.1 = ((bf16[64,4,256]{2,0,1:T(8,128)(2,1)}), bf16[64,4,256]{2,0,1:T(8,128)(2,1)S(1)}, u32[]{:S(2)}, u32[]{:S(2)}) async-start(bf16[64,4,256]{2,0,1:T(8,128)(2,1)} %bitcast.110), calls=%async_computation.1 | async-start | bytes 262144 | tf_op jit(solution)/shard_map/all_to_all | solution.py:22
  14.3 2.3 %copy.112 = bf16[8,4,8,2048]{3,2,0,1:T(8,128)(2,1)} copy(bf16[8,4,8,2048]{3,2,1,0:T(8,128)(2,1)} %bitcast.127) | data formatting | bytes 2097152 | tf_op jit(solution)/shard_map/all_to_all | solution.py:20
  16.6 2.7 %all-to-all-done.1 = bf16[64,4,256]{2,0,1:T(8,128)(2,1)S(1)} async-done(((bf16[64,4,256]{2,0,1:T(8,128)(2,1)}), bf16[64,4,256]{2,0,1:T(8,128)(2,1)S(1)}, u32[]{:S(2)}, u32[]{:S(2)}) %all-to-all-start.1) | async-done | bytes 131104 | tf_op jit(solution)/shard_map/all_to_all | solution.py:22
  19.3 3.5 %all-to-all-start.2 = ((bf16[64,4,2048]{2,0,1:T(8,128)(2,1)}), bf16[64,4,2048]{2,0,1:T(8,128)(2,1)S(1)}, u32[]{:S(2)}, u32[]{:S(2)}) async-start(bf16[64,4,2048]{2,0,1:T(8,128)(2,1)} %bitcast.109), calls=%async_computation.2 | async-start | bytes 2097152 | tf_op jit(solution)/shard_map/all_to_all | solution.py:20
  24.8 2.3 %copy.111 = bf16[8,4,8,2048]{3,2,0,1:T(8,128)(2,1)} copy(bf16[8,4,8,2048]{3,2,1,0:T(8,128)(2,1)} %bitcast.128) | data formatting | bytes 2097152 | tf_op jit(solution)/shard_map/all_to_all | solution.py:23
  27.1 7.0 %all-to-all-done.2 = bf16[64,4,2048]{2,0,1:T(8,128)(2,1)S(1)} async-done(((bf16[64,4,2048]{2,0,1:T(8,128)(2,1)}), bf16[64,4,2048]{2,0,1:T(8,128)(2,1)S(1)}, u32[]{:S(2)}, u32[]{:S(2)}) %all-to-all-start.2) | async-done | bytes 1048608 | tf_op jit(solution)/shard_map/all_to_all | solution.py:20
  34.1 3.5 %all-to-all-start.3 = ((bf16[64,4,2048]{2,0,1:T(8,128)(2,1)}), bf16[64,4,2048]{2,0,1:T(8,128)(2,1)S(1)}, u32[]{:S(2)}, u32[]{:S(2)}) async-start(bf16[64,4,2048]{2,0,1:T(8,128)(2,1)} %bitcast.108), calls=%async_computation.3 | async-start | bytes 2097152 | tf_op jit(solution)/shard_map/all_to_all | solution.py:23
  37.7 1.9 %collective-permute-start.1 = (bf16[2,256,256]{2,1,0:T(8,128)(2,1)S(1)}, bf16[2,256,256]{2,1,0:T(8,128)(2,1)}, u32[]{:S(2)}, u32[]{:S(2)}) collective-permute-start(bf16[2,256,256]{2,1,0:T(8,128)(2,1)S(1)} %collective-permute-done), channel_id=1, source_target_pairs={{0,4},{4,8},{8,12},{12,16},{16,20},{20,24},{24,28},{1,5},{5,9},{9,... | collective-permute-start | bytes 786440 | tf_op jit(solution)/shard_map/ppermute | solution.py:12
  39.7 5.7 %collective-permute-done.1 = bf16[2,256,256]{2,1,0:T(8,128)(2,1)} collective-permute-done((bf16[2,256,256]{2,1,0:T(8,128)(2,1)S(1)}, bf16[2,256,256]{2,1,0:T(8,128)(2,1)}, u32[]{:S(2)}, u32[]{:S(2)}) %collective-permute-start.1) | collective-permute-done | bytes 262176 | tf_op jit(solution)/shard_map/ppermute | solution.py:12
  57.1 2.1 %copy.63 = bf16[1,1024,256]{1,2,0:T(8,128)(2,1)} copy(bf16[1,1024,256]{2,1,0:T(8,128)(2,1)} %get-tuple-element.4) | data formatting | bytes 1048576 | tf_op jit(solution)/shard_map/slice | solution.py:34
  59.2 9.6 %fusion.23 = (f32[2,8,256]{2,1,0:T(8,128)S(1)}, f32[2,8,256,1024]{2,3,1,0:T(8,128)}) fusion(pred[256,1024]{0,1:T(8,128)(4,1)S(1)} %copy-done.3, bf16[1024,2,128,1]{0,2,3,1:T(8,128)(2,1)} %bitcast.121, bf16[256,2,8,128]{0,3,2,1:T(8,128)(2,1)S(1)} %copy.77), kind=kOutput, calls=%fused_computation.49 | convolution fusion | flops 1090520064 | bytes 18628608 | tf_op jit(solution)/shard_map/sub | solution.py:60
  68.8 6.6 %fusion.7 = bf16[2,8,256,1024]{2,3,1,0:T(8,128)(2,1)S(1)} fusion(f32[2,8,256,1024]{2,3,1,0:T(8,128)} %get-tuple-element.15, f32[2,8,256]{2,1,0:T(8,128)S(1)} %get-tuple-element.14), kind=kLoop, calls=%fused_computation.11 | loop fusion | flops 8388608 | bytes 25182208 | tf_op jit(solution)/shard_map/convert_element_type | solution.py:62
  75.4 3.8 %fusion.24 = f32[2,1024,128,1]{1,2,3,0:T(8,128)} fusion(bf16[2,8,256,1024]{2,3,1,0:T(8,128)(2,1)S(1)} %fusion.7, bf16[256,2,8,128]{0,3,2,1:T(8,128)(2,1)S(1)} %copy.71), kind=kOutput, calls=%fused_computation.50 | convolution fusion | flops 1073741824 | bytes 10485760 | tf_op jit(solution)/shard_map/kgij,ikgd->jkd/dot_general | solution.py:68
  82.1 7.1 %fusion.2 = bf16[2,8,256,1024]{2,3,1,0:T(8,128)(2,1)S(1)} fusion(f32[2,8,256]{2,1,0:T(8,128)S(1)} %bitcast.135, f32[2,8,256,1024]{2,3,1,0:T(8,128)} %get-tuple-element.15, f32[2,8,256]{2,1,0:T(8,128)S(1)} %get-tuple-element.14, bf16[1024,2,128,1]{0,2,3,1:T(8,128)(2,1)S(1)} %bitcast.119, bf16[256,2,8,128]{0,3,2,1:T(8,128)(2,1)S(1)} %copy.71), kind=kOutput, calls=%fused_computation.3 | convolution fusion | flops 1090519040 | bytes 26771456 | tf_op jit(solution)/shard_map/ikgd,jkd->kgij/dot_general | solution.py:71
  89.2 3.2 %copy-done = bf16[2,8,256,1024]{2,3,1,0:T(8,128)(2,1)} copy-done((bf16[2,8,256,1024]{2,3,1,0:T(8,128)(2,1)}, bf16[2,8,256,1024]{2,3,1,0:T(8,128)(2,1)S(1)}, u32[]{:S(2)}) %copy-start) | copy-done | bytes 8388632
  92.5 5.1 %fusion.11 = f32[2,1024,128]{1,2,0:T(8,128)} fusion(bf16[2,8,256,1024]{2,3,1,0:T(8,128)(2,1)S(1)} %fusion.2, bf16[256,2,8,128]{0,3,2,1:T(8,128)(2,1)} %copy-done.1), kind=kOutput, calls=%fused_computation.23 | convolution fusion | flops 1074003968 | bytes 10485760 | tf_op jit(solution)/shard_map/kgij,ikgd->jkd/dot_general | solution.py:80
  100.0 3.1 %collective-permute-start.3 = (f32[2,256,256]{2,1,0:T(8,128)}, f32[2,256,256]{2,1,0:T(8,128)}, u32[]{:S(2)}, u32[]{:S(2)}) collective-permute-start(f32[2,256,256]{2,1,0:T(8,128)} %fusion.14), channel_id=1, source_target_pairs={{4,0},{8,4},{12,8},{16,12},{20,16},{24,20},{28,24},{5,1},{9,5},{13... | collective-permute-start | bytes 1572872 | tf_op jit(solution)/shard_map/ppermute | solution.py:12
  103.2 6.0 %multiply_bitcast_fusion = f32[256,2,8,128]{0,3,2,1:T(8,128)} fusion(bf16[1024,2,128,1]{0,2,3,1:T(8,128)(2,1)S(1)} %bitcast.122, bf16[2,8,256,1024]{2,3,1,0:T(8,128)(2,1)} %copy-done), kind=kOutput, calls=%fused_computation.20 | convolution fusion | flops 1074266112 | bytes 11010048 | tf_op jit(solution)/shard_map/kgij,jkd->ikgd/dot_general | solution.py:76
  109.2 3.0 %copy.74 = f32[256,2,8,128]{3,2,1,0:T(8,128)} copy(f32[256,2,8,128]{0,3,2,1:T(8,128)} %multiply_bitcast_fusion) | data formatting | bytes 4194304 | tf_op jit(solution)/shard_map/mul | solution.py:76
  112.2 2.7 %all_to_all.91 = f32[4,64,2048]{2,1,0:T(8,128)} reshape(f32[256,2,8,128]{3,2,1,0:T(8,128)} %copy.74) | data formatting | bytes 4194304 | tf_op jit(solution)/shard_map/all_to_all | solution.py:93
  114.9 4.5 %all-to-all-start.4 = ((f32[4,64,2048]{2,1,0:T(8,128)}), f32[4,64,2048]{2,1,0:T(8,128)}, u32[]{:S(2)}, u32[]{:S(2)}) async-start(f32[4,64,2048]{2,1,0:T(8,128)} %all_to_all.91), calls=%async_computation.4 | async-start | bytes 4194304 | tf_op jit(solution)/shard_map/all_to_all | solution.py:93
  120.5 1.9 %collective-permute-start.4 = (f32[2,256,256]{2,1,0:T(8,128)S(1)}, f32[2,256,256]{2,1,0:T(8,128)S(1)}, u32[]{:S(2)}, u32[]{:S(2)}) collective-permute-start(f32[2,256,256]{2,1,0:T(8,128)S(1)} %fusion.16), channel_id=1, source_target_pairs={{4,0},{8,4},{12,8},{16,12},{20,16},{24,20},{28,24},{5,1},{9,5},{13... | collective-permute-start | bytes 1572872 | tf_op jit(solution)/shard_map/ppermute | solution.py:12
  122.4 6.7 %collective-permute-done.4 = f32[2,256,256]{2,1,0:T(8,128)S(1)} collective-permute-done((f32[2,256,256]{2,1,0:T(8,128)S(1)}, f32[2,256,256]{2,1,0:T(8,128)S(1)}, u32[]{:S(2)}, u32[]{:S(2)}) %collective-permute-start.4) | collective-permute-done | bytes 524320 | tf_op jit(solution)/shard_map/ppermute | solution.py:12
  129.2 4.2 %collective-permute-start.5 = (f32[2,256,256]{2,1,0:T(8,128)S(1)}, f32[2,256,256]{2,1,0:T(8,128)S(1)}, u32[]{:S(2)}, u32[]{:S(2)}) collective-permute-start(f32[2,256,256]{2,1,0:T(8,128)S(1)} %fusion.13), channel_id=1, source_target_pairs={{4,0},{8,4},{12,8},{16,12},{20,16},{24,20},{28,24},{5,1},{9,5},{13... | collective-permute-start | bytes 1572872 | tf_op jit(solution)/shard_map/ppermute | solution.py:12
  133.4 6.7 %collective-permute-done.5 = f32[2,256,256]{2,1,0:T(8,128)S(1)} collective-permute-done((f32[2,256,256]{2,1,0:T(8,128)S(1)}, f32[2,256,256]{2,1,0:T(8,128)S(1)}, u32[]{:S(2)}, u32[]{:S(2)}) %collective-permute-start.5) | collective-permute-done | bytes 524320 | tf_op jit(solution)/shard_map/ppermute | solution.py:12
  140.9 4.0 %all-to-all-done.4 = f32[4,64,2048]{2,1,0:T(8,128)} async-done(((f32[4,64,2048]{2,1,0:T(8,128)}), f32[4,64,2048]{2,1,0:T(8,128)}, u32[]{:S(2)}, u32[]{:S(2)}) %all-to-all-start.4) | async-done | bytes 2097184 | tf_op jit(solution)/shard_map/all_to_all | solution.py:93
  144.9 3.4 %all-to-all-start.6 = ((f32[4,64,256]{2,1,0:T(8,128)}), f32[4,64,256]{2,1,0:T(8,128)S(1)}, u32[]{:S(2)}, u32[]{:S(2)}) async-start(f32[4,64,256]{2,1,0:T(8,128)} %bitcast.29), calls=%async_computation.6 | async-start | bytes 524288 | tf_op jit(solution)/shard_map/all_to_all | solution.py:100
  149.1 4.6 %all-to-all-done.6 = f32[4,64,256]{2,1,0:T(8,128)S(1)} async-done(((f32[4,64,256]{2,1,0:T(8,128)}), f32[4,64,256]{2,1,0:T(8,128)S(1)}, u32[]{:S(2)}, u32[]{:S(2)}) %all-to-all-start.6) | async-done | bytes 262176 | tf_op jit(solution)/shard_map/all_to_all | solution.py:100
  153.6 3.4 %all-to-all-start.5 = ((f32[4,64,256]{2,1,0:T(8,128)}), f32[4,64,256]{2,1,0:T(8,128)S(1)}, u32[]{:S(2)}, u32[]{:S(2)}) async-start(f32[4,64,256]{2,1,0:T(8,128)} %pad_maximum_fusion.2), calls=%async_computation.5 | async-start | bytes 524288 | tf_op jit(solution)/shard_map/all_to_all | solution.py:95
  157.1 3.1 %copy.102 = f32[4,8,8,2048]{3,2,0,1:T(8,128)} copy(f32[4,8,8,2048]{3,2,1,0:T(8,128)} %bitcast.52) | data formatting | bytes 4194304 | tf_op jit(solution)/shard_map/all_to_all | solution.py:93
  (45 shorter events, 27.8 us)
Async XLA Ops:
  0.6 39.0 %copy-start.5 = (s32[2048]{0:T(1024)S(1)}, s32[2048]{0:T(1024)}, u32[]{:S(2)}) copy-start(s32[2048]{0:T(1024)} %param.9) | copy-start | bytes 24580
  2.2 8.7 %all-to-all-start = ((bf16[64,4,256]{2,0,1:T(8,128)(2,1)}), bf16[64,4,256]{2,0,1:T(8,128)(2,1)S(1)}, u32[]{:S(2)}, u32[]{:S(2)}) async-start(bf16[64,4,256]{2,0,1:T(8,128)(2,1)} %bitcast.111), calls=%async_computation | async-start | bytes 262144 | tf_op jit(solution)/shard_map/all_to_all | solution.py:21
  11.0 8.3 %all-to-all-start.1 = ((bf16[64,4,256]{2,0,1:T(8,128)(2,1)}), bf16[64,4,256]{2,0,1:T(8,128)(2,1)S(1)}, u32[]{:S(2)}, u32[]{:S(2)}) async-start(bf16[64,4,256]{2,0,1:T(8,128)(2,1)} %bitcast.110), calls=%async_computation.1 | async-start | bytes 262144 | tf_op jit(solution)/shard_map/all_to_all | solution.py:22
  19.3 14.8 %all-to-all-start.2 = ((bf16[64,4,2048]{2,0,1:T(8,128)(2,1)}), bf16[64,4,2048]{2,0,1:T(8,128)(2,1)S(1)}, u32[]{:S(2)}, u32[]{:S(2)}) async-start(bf16[64,4,2048]{2,0,1:T(8,128)(2,1)} %bitcast.109), calls=%async_computation.2 | async-start | bytes 2097152 | tf_op jit(solution)/shard_map/all_to_all | solution.py:20
  22.8 14.8 %collective-permute-start = (bf16[2,256,256]{2,1,0:T(8,128)(2,1)S(1)}, bf16[2,256,256]{2,1,0:T(8,128)(2,1)S(1)}, u32[]{:S(2)}, u32[]{:S(2)}) collective-permute-start(bf16[2,256,256]{2,1,0:T(8,128)(2,1)S(1)} %pad_maximum_fusion.1), channel_id=1, source_target_pairs={{0,4},{4,8},{8,12},{12,16},{16,20},{20,24},{24,28},{1,5},{5,9},{9,... | collective-permute-start | bytes 786440 | tf_op jit(solution)/shard_map/ppermute | solution.py:12
  34.1 16.6 %all-to-all-start.3 = ((bf16[64,4,2048]{2,0,1:T(8,128)(2,1)}), bf16[64,4,2048]{2,0,1:T(8,128)(2,1)S(1)}, u32[]{:S(2)}, u32[]{:S(2)}) async-start(bf16[64,4,2048]{2,0,1:T(8,128)(2,1)} %bitcast.108), calls=%async_computation.3 | async-start | bytes 2097152 | tf_op jit(solution)/shard_map/all_to_all | solution.py:23
  37.6 11.3 %copy-start.4 = (bf16[2,256,256]{2,1,0:T(8,128)(2,1)}, bf16[2,256,256]{2,1,0:T(8,128)(2,1)S(1)}, u32[]{:S(2)}) copy-start(bf16[2,256,256]{2,1,0:T(8,128)(2,1)S(1)} %collective-permute-done) | copy-start | bytes 786436
  37.7 7.8 %collective-permute-start.1 = (bf16[2,256,256]{2,1,0:T(8,128)(2,1)S(1)}, bf16[2,256,256]{2,1,0:T(8,128)(2,1)}, u32[]{:S(2)}, u32[]{:S(2)}) collective-permute-start(bf16[2,256,256]{2,1,0:T(8,128)(2,1)S(1)} %collective-permute-done), channel_id=1, source_target_pairs={{0,4},{4,8},{8,12},{12,16},{16,20},{20,24},{24,28},{1,5},{5,9},{9,... | collective-permute-start | bytes 786440 | tf_op jit(solution)/shard_map/ppermute | solution.py:12
  45.4 8.2 %collective-permute-start.2 = (bf16[2,256,256]{2,1,0:T(8,128)(2,1)}, bf16[2,256,256]{2,1,0:T(8,128)(2,1)}, u32[]{:S(2)}, u32[]{:S(2)}) collective-permute-start(bf16[2,256,256]{2,1,0:T(8,128)(2,1)} %collective-permute-done.1), channel_id=1, source_target_pairs={{0,4},{4,8},{8,12},{12,16},{16,20},{20,24},{24,28},{1,5},{5,9},{9,... | collective-permute-start | bytes 786440 | tf_op jit(solution)/shard_map/ppermute | solution.py:12
  50.0 18.8 %copy-start.1 = (bf16[256,2,8,128]{0,3,2,1:T(8,128)(2,1)}, bf16[256,2,8,128]{0,3,2,1:T(8,128)(2,1)S(1)}, u32[]{:S(2)}) copy-start(bf16[256,2,8,128]{0,3,2,1:T(8,128)(2,1)S(1)} %copy.77) | copy-start | bytes 3145732
  51.9 7.2 %copy-start.3 = (pred[256,1024]{0,1:T(8,128)(4,1)S(1)}, pred[256,1024]{0,1:T(8,128)(4,1)}, u32[]{:S(2)}) copy-start(pred[256,1024]{0,1:T(8,128)(4,1)} %compare_and_fusion) | copy-start | bytes 786436
  89.2 3.3 %copy-start = (bf16[2,8,256,1024]{2,3,1,0:T(8,128)(2,1)}, bf16[2,8,256,1024]{2,3,1,0:T(8,128)(2,1)S(1)}, u32[]{:S(2)}) copy-start(bf16[2,8,256,1024]{2,3,1,0:T(8,128)(2,1)S(1)} %fusion.2) | copy-start | bytes 25165828
  92.5 10.7 %copy-start.2 = (bf16[1,1024,256]{1,2,0:T(8,128)(2,1)S(1)}, bf16[1,1024,256]{1,2,0:T(8,128)(2,1)}, u32[]{:S(2)}) copy-start(bf16[1,1024,256]{1,2,0:T(8,128)(2,1)} %copy.63) | copy-start | bytes 1572868
  100.0 19.4 %collective-permute-start.3 = (f32[2,256,256]{2,1,0:T(8,128)}, f32[2,256,256]{2,1,0:T(8,128)}, u32[]{:S(2)}, u32[]{:S(2)}) collective-permute-start(f32[2,256,256]{2,1,0:T(8,128)} %fusion.14), channel_id=1, source_target_pairs={{4,0},{8,4},{12,8},{16,12},{20,16},{24,20},{28,24},{5,1},{9,5},{13... | collective-permute-start | bytes 1572872 | tf_op jit(solution)/shard_map/ppermute | solution.py:12
  114.9 30.0 %all-to-all-start.4 = ((f32[4,64,2048]{2,1,0:T(8,128)}), f32[4,64,2048]{2,1,0:T(8,128)}, u32[]{:S(2)}, u32[]{:S(2)}) async-start(f32[4,64,2048]{2,1,0:T(8,128)} %all_to_all.91), calls=%async_computation.4 | async-start | bytes 4194304 | tf_op jit(solution)/shard_map/all_to_all | solution.py:93
  120.5 8.6 %collective-permute-start.4 = (f32[2,256,256]{2,1,0:T(8,128)S(1)}, f32[2,256,256]{2,1,0:T(8,128)S(1)}, u32[]{:S(2)}, u32[]{:S(2)}) collective-permute-start(f32[2,256,256]{2,1,0:T(8,128)S(1)} %fusion.16), channel_id=1, source_target_pairs={{4,0},{8,4},{12,8},{16,12},{20,16},{24,20},{28,24},{5,1},{9,5},{13... | collective-permute-start | bytes 1572872 | tf_op jit(solution)/shard_map/ppermute | solution.py:12
  129.2 10.9 %collective-permute-start.5 = (f32[2,256,256]{2,1,0:T(8,128)S(1)}, f32[2,256,256]{2,1,0:T(8,128)S(1)}, u32[]{:S(2)}, u32[]{:S(2)}) collective-permute-start(f32[2,256,256]{2,1,0:T(8,128)S(1)} %fusion.13), channel_id=1, source_target_pairs={{4,0},{8,4},{12,8},{16,12},{20,16},{24,20},{28,24},{5,1},{9,5},{13... | collective-permute-start | bytes 1572872 | tf_op jit(solution)/shard_map/ppermute | solution.py:12
  144.9 8.8 %all-to-all-start.6 = ((f32[4,64,256]{2,1,0:T(8,128)}), f32[4,64,256]{2,1,0:T(8,128)S(1)}, u32[]{:S(2)}, u32[]{:S(2)}) async-start(f32[4,64,256]{2,1,0:T(8,128)} %bitcast.29), calls=%async_computation.6 | async-start | bytes 524288 | tf_op jit(solution)/shard_map/all_to_all | solution.py:100
  153.6 8.8 %all-to-all-start.5 = ((f32[4,64,256]{2,1,0:T(8,128)}), f32[4,64,256]{2,1,0:T(8,128)S(1)}, u32[]{:S(2)}, u32[]{:S(2)}) async-start(f32[4,64,256]{2,1,0:T(8,128)} %pad_maximum_fusion.2), calls=%async_computation.5 | async-start | bytes 524288 | tf_op jit(solution)/shard_map/all_to_all | solution.py:95
